TPU v7x, 32 devices: a whole 2x2x4 slice. The times are simulated.
32 devices in a mesh: grp: 2 (over y), tgt: 4 (over z), src: 4 (over x, core).
Axes of the slice: x: 2, y: 2, z: 4, core: 2. Of those that a mesh axis runs over, the one named last changes fastest.
Arguments:
- target_rows: bfloat16 [2048, 4608], P(('grp', 'tgt', 'src')), parts along dimension 0, may hold values from -6 to 6
- target_pos: int32 [2048], P(('grp', 'tgt')), parts along dimension 0, may hold values from 0 to 255
- decoder_rows: bfloat16 [512, 4608], P(('grp', 'tgt', 'src')), parts along dimension 0, may hold values from -0.09375 to 0.09375
- source_pos: int32 [512], P('grp'), parts along dimension 0, may hold values from 0 to 255
- out_proj: bfloat16 [32, 4608, 128], P('src', 'tgt'), may hold values from -0.09375 to 0.09375
- value_proj: bfloat16 [16, 4608, 128], P('src'), may hold values from -1 to 1
- attention: bfloat16 [64, 256, 256], P(('grp', 'src'), 'tgt'), parts along dimension 0, may hold values from 0 to 1, as said below
- tile_pattern: int32 [8, 4], P('grp'), parts along dimension 0, may hold values from 0 to 1, as said below
Outputs:
- edges: bfloat16 [512, 1024], P(('grp', 'src'), 'tgt'), parts along dimension 0
There are 2 independent parts, one for each index of `grp`. A program takes and returns all parts, laid end to end along the dimension named above; an argument that names none is the same for every part. Nothing has to cross between parts.
Inputs may be any that keep to these rules, and one draw needn't show every extreme that they name: Each row attention[h, p, :] is a probability distribution over the keys 0 to p: zero beyond p, summing to one. tile_pattern[b, c] is 1 where the tile of edges between source block b and target block c is kept, else 0.
All inputs are finite; a program needn't handle non-finite values.
Results may differ from a plain program's by a relative error of at most 0.0057.
Values may be sent and summed in bfloat16 or wider, within the bound.
A program may use at most 64 MiB of HBM per device.

v0:
```python
import functools

import jax
import jax.numpy as jnp
from jax import lax
from jax.experimental import pallas as pl
from jax.experimental.pallas import tpu as pltpu
from jax.sharding import PartitionSpec as P


def passed_along(value, axis, steps):
    count = lax.axis_size(axis)
    pairs = [(source, (source + steps) % count) for source in range(count)]
    return lax.ppermute(value, axis, pairs)


def gathered_shards(
    target_rows, target_pos, decoder_rows, source_pos, out_proj, value_proj, attention, tile_pattern
):
    blocks = lax.axis_size("tgt")
    column = lax.axis_index("tgt")
    src_lane = lax.axis_index("src")
    full_targets, full_sources = (
        lax.all_gather(target_rows, "src", axis=0, tiled=True),
        lax.all_gather(decoder_rows, "src", axis=0, tiled=True),
    )
    tgt_dev = full_targets.shape[0]
    src_dev = full_sources.shape[0]
    sub_rows = decoder_rows.shape[0]
    heads_here = out_proj.shape[0]
    head_dim = out_proj.shape[2]
    groups_here = value_proj.shape[0]
    repeat = heads_here // groups_here
    read_sum = jnp.einsum(
        "td,hde->the",
        full_targets,
        lax.all_gather(out_proj, "tgt", axis=1, tiled=True),
        preferred_element_type=jnp.float32,
    )
    head_reads = read_sum.astype(jnp.bfloat16).reshape(tgt_dev, groups_here, repeat, head_dim)
    values = jnp.einsum("sd,gde->sge", full_sources, value_proj, preferred_element_type=jnp.float32)
    values = values.astype(jnp.bfloat16).reshape(src_dev, groups_here * head_dim)
    attn_table = lax.all_gather(attention, "tgt", axis=1, tiled=True)
    target_attn = jnp.take(attn_table, target_pos, axis=1)
    keyed_attn = jnp.transpose(target_attn, (0, 2, 1))

    def edge_tile(payload, block_index):
        decoder_part, value_part = payload
        key_positions = lax.dynamic_slice_in_dim(source_pos, block_index * src_dev, src_dev)
        weights = jnp.take(keyed_attn, key_positions, axis=1).astype(jnp.float32)
        scores = jnp.einsum(
            "sgd,tgrd->grst",
            value_part.reshape(src_dev, groups_here, head_dim),
            head_reads,
            preferred_element_type=jnp.float32,
        )
        scores = scores.reshape(heads_here, src_dev, tgt_dev)
        mixed_term = jnp.sum(weights * scores, axis=0)
        own_positions = lax.dynamic_slice_in_dim(key_positions, src_lane * sub_rows, sub_rows)
        same_place = (own_positions[:, None] == target_pos[None, :]).astype(jnp.float32)
        direct = (
            jnp.einsum("sd,td->st", decoder_part, full_targets, preferred_element_type=jnp.float32)
            * same_place
        )
        own_rows = lax.dynamic_slice_in_dim(mixed_term, src_lane * sub_rows, sub_rows, 0)
        return lax.dynamic_update_slice_in_dim(
            mixed_term, own_rows + direct, src_lane * sub_rows, 0
        )

    def place_tile(partial_value, payload, block_index):
        kept_flag = tile_pattern[block_index, column]
        piece_tile = edge_tile(payload, block_index) * kept_flag.astype(jnp.float32)
        return lax.dynamic_update_slice_in_dim(partial_value, piece_tile, block_index * src_dev, 0)

    own_block = (decoder_rows, values)
    partial_value = jnp.zeros((blocks * src_dev, tgt_dev), jnp.float32)
    partial_value = place_tile(partial_value, own_block, column)

    def cycle_turn(turn_index, state_carry):
        forward_block, backward_block, running = state_carry
        forward_block = passed_along((forward_block[0], forward_block[1]), "tgt", 1)
        backward_block = passed_along((backward_block[0], backward_block[1]), "tgt", -1)
        running = place_tile(running, forward_block, (column - turn_index) % blocks)
        running = place_tile(running, backward_block, (column + turn_index) % blocks)
        return (forward_block, backward_block, running)

    forward_block, backward_block, partial_value = lax.fori_loop(
        1, blocks // 2, cycle_turn, (own_block, own_block, partial_value)
    )
    forward_block = passed_along((forward_block[0], forward_block[1]), "tgt", 1)
    partial_value = place_tile(partial_value, forward_block, (column - blocks // 2) % blocks)
    summed = lax.psum_scatter(partial_value, "src", scatter_dimension=0, tiled=True)
    return summed.astype(jnp.bfloat16)


F32 = jnp.float32
BF16 = jnp.bfloat16
MESH = pl.DeviceIdType.MESH


def dot(a, b):
    return jnp.dot(a, b, preferred_element_type=F32)


def dot_nt(a, b):
    return lax.dot_general(a, b, (((1,), (1,)), ((), ())), preferred_element_type=F32)


def edge_kernel(
    nt, ns, tgt_ref, tpos_ref, dec_ref, srow_ref, oproj_hbm, vproj_hbm, attn_ref, pat_ref,
    out_ref,
    oproj, vproj, tslices, dslices, decfull, attn, tpos, values, reads, attn_n, onehot, edges,
    core_in, x_out, x_in, z_out, z_in, scol_ref,
    local_sem, zt_s, zt_r, zd_s, zd_r, zp_s, zp_r, ar_s, al_s, a_r, vr_s, vl_s, v_r,
    xt_s, xt_r, ct_s, ct_r, xf_s, xf_r, cf_s, cf_r, ce_s, ce_r, xe_s, xe_r, ze_s, ze_r,
):
    c = lax.axis_index("tgt")
    s = lax.axis_index("src")
    nx = ns // 2
    x = s // 2
    core = s % 2
    mate = x * 2 + 1 - core
    rows, depth = tslices.shape[1] // ns, tslices.shape[2]
    sub = dec_ref.shape[0]
    heads = oproj.shape[0]
    groups = vproj.shape[0]
    block = sub * ns
    queries, keys = attn_ref.shape[1:]
    targets = tpos.shape[2]
    total = scol_ref.shape[0]
    own = edges.shape[1] // ns

    def zdev(k):
        return lax.rem(c + k, nt)

    def xsrc(dx):
        return lax.rem(x + dx, nx) * 2 + core

    def xother(dx):
        return lax.rem(x + dx, nx) * 2 + 1 - core

    sent = []

    def send(src, dst, ssem, rsem, axis, index):
        cp = pltpu.make_async_remote_copy(
            src_ref=src, dst_ref=dst, send_sem=ssem, recv_sem=rsem,
            device_id={axis: index}, device_id_type=MESH,
        )
        cp.start()
        sent.append(cp)

    def arrived(dst, rsem):
        pltpu.make_async_remote_copy(
            src_ref=dst, dst_ref=dst, send_sem=local_sem.at[0], recv_sem=rsem,
            device_id={"src": mate}, device_id_type=MESH,
        ).wait_recv()

    barrier = pltpu.get_barrier_semaphore()
    for k in range(1, nt):
        pl.semaphore_signal(barrier, inc=1, device_id={"tgt": zdev(k)}, device_id_type=MESH)
    for dx in range(1, nx):
        pl.semaphore_signal(barrier, inc=1, device_id={"src": xsrc(dx)}, device_id_type=MESH)
        pl.semaphore_signal(barrier, inc=1, device_id={"src": xother(dx)}, device_id_type=MESH)
    pl.semaphore_signal(barrier, inc=1, device_id={"src": mate}, device_id_type=MESH)
    fetch_v = pltpu.make_async_copy(vproj_hbm, vproj, local_sem.at[1])
    fetch_o = pltpu.make_async_copy(oproj_hbm, oproj, local_sem.at[2])
    fetch_v.start()
    fetch_o.start()
    pl.semaphore_wait(barrier, nt - 1 + ns - 1)

    def cols(b):
        return pl.ds(pl.multiple_of(b * depth, 128), depth)

    def trow(lane):
        return pl.ds(pl.multiple_of(lane * rows, rows), rows)

    def drow(lane):
        return pl.ds(pl.multiple_of(lane * sub, sub), sub)

    def qrow(b):
        return pl.ds(pl.multiple_of(b * queries, queries), queries)

    def vrow(b):
        return pl.ds(pl.multiple_of(b * block, block), block)

    def erow(lane):
        return pl.ds(pl.multiple_of(lane * own, own), own)

    for dx in range(1, nx):
        send(dec_ref, decfull.at[drow(s)], xf_s.at[dx], xf_r.at[x], "src", xsrc(dx))
    send(dec_ref, decfull.at[drow(s)], cf_s.at[0], cf_r.at[x], "src", mate)
    def spread(k):
        b = zdev(k)
        send(tgt_ref.at[:, cols(b)], tslices.at[c, trow(s)], zt_s.at[k], zt_r.at[c], "tgt", b)
        send(dec_ref.at[:, cols(b)], dslices.at[drow(c)], zd_s.at[k], zd_r.at[c], "tgt", b)
        send(tpos_ref, tpos.at[c], zp_s.at[k], zp_r.at[c], "tgt", b)

    for dx in range(1, nx):
        send(tgt_ref.at[:, cols(c)], tslices.at[c, trow(s)], xt_s.at[0, dx], xt_r.at[c, x], "src", xsrc(dx))
    send(tgt_ref.at[:, cols(c)], tslices.at[c, trow(s)], ct_s.at[0, 0], ct_r.at[c, x], "src", mate)

    half = keys // 2
    lowest = half // queries if half % 128 == 0 else 0

    def attn_copy(src, b, ssem, device, act):
        @pl.when(b < lowest)
        def _():
            act(pltpu.make_async_remote_copy(
                src_ref=src.at[:, :, pl.ds(0, half)], dst_ref=attn.at[:, qrow(b), pl.ds(0, half)],
                send_sem=ssem.at[b], recv_sem=a_r.at[b],
                device_id={"tgt": device}, device_id_type=MESH,
            ))

        @pl.when(b >= lowest)
        def _():
            act(pltpu.make_async_remote_copy(
                src_ref=src, dst_ref=attn.at[:, qrow(b), :],
                send_sem=ssem.at[b], recv_sem=a_r.at[b],
                device_id={"tgt": device}, device_id_type=MESH,
            ))

    def value_copy(b, ssem, device):
        return pltpu.make_async_remote_copy(
            src_ref=values.at[:, vrow(b), :], dst_ref=values.at[:, vrow(b), :],
            send_sem=ssem.at[b], recv_sem=v_r.at[b],
            device_id={"tgt": device}, device_id_type=MESH,
        )

    start = lambda copy: copy.start()
    wait_send = lambda copy: copy.wait_send()
    wait_recv = lambda copy: copy.wait_recv()

    @pl.when(c + 1 < nt)
    def _():
        attn_copy(attn_ref, c, ar_s, c + 1, start)

    @pl.when(c > 0)
    def _():
        attn_copy(attn_ref, c, al_s, c - 1, start)

    spread(1)
    spread(2)

    for b in range(lowest):
        attn[:, b * queries:(b + 1) * queries, half:] = jnp.zeros((heads, queries, keys - half), BF16)
    scol_ref[...] = jnp.transpose(jnp.broadcast_to(srow_ref[...], (128, total)))[:, :1]
    tslices[c, trow(s)] = tgt_ref[:, cols(c)]
    dslices[drow(c)] = dec_ref[:, cols(c)]
    decfull[drow(s)] = dec_ref[...]
    tpos[c] = tpos_ref[...]
    attn[:, qrow(c), :] = attn_ref[...]

    for dx in range(1, nx):
        y = xsrc(dx)
        arrived(decfull.at[drow(y)], xf_r.at[lax.rem(x + dx, nx)])
        send(decfull.at[drow(y)], decfull.at[drow(y)], cf_s.at[dx], cf_r.at[lax.rem(x + dx, nx)], "src", mate)
    for dx in range(nx):
        z = lax.rem(x + dx, nx)
        arrived(decfull.at[drow(z * 2 + 1 - core)], cf_r.at[z])
    fetch_v.wait()

    @pl.loop(0, groups)
    def _(g):
        values[g, vrow(c)] = dot(decfull[...], vproj[g]).astype(BF16)

    @pl.when(c + 1 < nt)
    def _():
        value_copy(c, vr_s, c + 1).start()

    @pl.when(c > 0)
    def _():
        value_copy(c, vl_s, c - 1).start()

    fetch_o.wait()

    def pass_rows(k):
        b = zdev(nt - k)
        arrived(tslices.at[b, trow(s)], zt_r.at[b])
        for dx in range(1, nx):
            send(tslices.at[b, trow(s)], tslices.at[b, trow(s)], xt_s.at[k, dx], xt_r.at[b, x], "src", xsrc(dx))
        send(tslices.at[b, trow(s)], tslices.at[b, trow(s)], ct_s.at[k, 0], ct_r.at[b, x], "src", mate)

    def pass_over(k):
        b = zdev(nt - k) if k else c
        for dx in range(1, nx):
            z = lax.rem(x + dx, nx)
            y = z * 2 + core
            arrived(tslices.at[b, trow(y)], xt_r.at[b, z])
            send(tslices.at[b, trow(y)], tslices.at[b, trow(y)], ct_s.at[k, dx], ct_r.at[b, z], "src", mate)

    def read_block(k):
        b = zdev(nt - k) if k else c
        for dx in range(nx):
            z = lax.rem(x + dx, nx)
            arrived(tslices.at[b, trow(z * 2 + 1 - core)], ct_r.at[b, z])

        @pl.loop(0, heads)
        def _(h):
            reads[b, h] = dot(tslices[b], oproj[h]).astype(BF16)

    def relay(k, copy_in, copy_on):
        @pl.when(c - k >= 0)
        def _():
            copy_in(c - k)

            @pl.when(c + 1 < nt)
            def _():
                copy_on(c - k, 0)

        @pl.when(c + k < nt)
        def _():
            copy_in(c + k)

            @pl.when(c > 0)
            def _():
                copy_on(c + k, 1)

    def attn_in(b):
        attn_copy(attn.at[:, qrow(b), :], b, ar_s, c, wait_recv)

    def attn_on(b, left):
        attn_copy(attn.at[:, qrow(b), :], b, al_s if left else ar_s, c - 1 if left else c + 1, start)

    def value_in(b):
        value_copy(b, vr_s, c).wait_recv()

    def value_on(b, left):
        value_copy(b, vl_s if left else vr_s, c - 1 if left else c + 1).start()

    def prepare(k):
        b = zdev(nt - k) if k else c
        if k:
            arrived(dslices.at[drow(b)], zd_r.at[b])
            arrived(tpos.at[b], zp_r.at[b])
        onehot[b] = (
            lax.broadcasted_iota(jnp.int32, (nt * queries, targets), 0) == tpos[b]
        ).astype(BF16)
        edges[b] = jnp.zeros(edges.shape[1:], F32)

    def add_direct(b):
        here = tpos[b]
        direct = dot_nt(dslices[...], tslices[b])
        for p in range(nt):
            at = pl.ds(pl.multiple_of(p * block + s * sub, sub), sub)
            same = (scol_ref[at] == here).astype(F32)
            edges[b, at] += direct[p * sub:(p + 1) * sub] * same

    def pick_keys():
        pick = (scol_ref[...] == lax.broadcasted_iota(jnp.int32, (total, keys), 1)).astype(BF16)

        @pl.loop(0, heads)
        def _(h):
            attn_n[h] = dot_nt(pick, attn[h]).astype(BF16)

    def tile(k):
        b = zdev(nt - 1 - k)
        repeat = heads // groups

        @pl.loop(0, groups)
        def _(g):
            terms = None
            for r in range(repeat):
                h = g * repeat + r
                term = dot(attn_n[h], onehot[b]) * dot_nt(values[g], reads[b, h])
                terms = term if terms is None else terms + term
            edges[b] += terms

        send(edges.at[b, erow(mate)], core_in.at[b], ce_s.at[k], ce_r.at[b], "src", mate)
        for dx in range(1, nx):
            for y in (xsrc(dx), xother(dx)):
                x_out[b, y] = edges[b, erow(y)].astype(BF16)
                send(x_out.at[b, y], x_in.at[b, s], xe_s.at[k, y], xe_r.at[b, s], "src", y)

    def over_z(k):
        b = zdev(nt - 1 - k)
        arrived(core_in.at[b], ce_r.at[b])
        mine = edges[b, erow(s)] + core_in[b]
        for dx in range(1, nx):
            for y in (xsrc(dx), xother(dx)):
                arrived(x_in.at[b, y], xe_r.at[b, y])
                mine += x_in[b, y].astype(F32)
        if k < nt - 1:
            z_out[b] = mine.astype(BF16)
            send(z_out.at[b], z_in.at[c], ze_s.at[k], ze_r.at[c], "tgt", b)
        return mine

    prepare(0)
    for k in range(1, nt):
        relay(k, attn_in, attn_on)
        if k == 1:
            for j in range(3, nt):
                spread(j)
        relay(k, value_in, value_on)
        if k == nt - 1:
            pick_keys()
        pass_rows(k)
        pass_over(k - 1)
        prepare(k)
        if k == 1:
            read_block(0)
    for k in range(1, nt + 2):
        if k < nt:
            read_block(k)
            add_direct(zdev(nt - k))
            tile(k - 1)
        if k == 1:
            pass_over(nt - 1)
        if k == nt:
            add_direct(c)
            tile(k - 1)
        if k > 1:
            mine = over_z(k - 2)
    for k in range(1, nt):
        b = zdev(k)
        arrived(z_in.at[b], ze_r.at[b])
        mine += z_in[b].astype(F32)
    kept = pat_ref[(s * own) // block, c]
    out_ref[...] = (mine * kept.astype(F32)).astype(BF16)

    for cp in sent:
        cp.wait_send()
    for k in range(nt):
        @pl.when((c - k >= 0) & (c + 1 < nt))
        def _():
            attn_copy(attn_ref, c - k, ar_s, c + 1, wait_send)
            value_copy(c - k, vr_s, c + 1).wait_send()

        @pl.when((c + k < nt) & (c > 0))
        def _():
            attn_copy(attn_ref, c + k, al_s, c - 1, wait_send)
            value_copy(c + k, vl_s, c - 1).wait_send()


def resident_shards(
    target_rows, target_pos, decoder_rows, source_pos, out_proj, value_proj, attention, tile_pattern
):
    nt, ns = lax.axis_size("tgt"), lax.axis_size("src")
    rows = target_rows.shape[0]
    sub, width = decoder_rows.shape
    heads, depth, head_dim = out_proj.shape
    groups = value_proj.shape[0]
    _, queries, keys = attention.shape
    total = source_pos.shape[0]
    targets = target_pos.shape[0]
    own = total // ns
    nx = ns // 2
    vmem = pl.BlockSpec(memory_space=pltpu.VMEM)
    hbm = pl.BlockSpec(memory_space=pl.ANY)
    sem = lambda *shape: pltpu.SemaphoreType.DMA(shape)
    return pl.pallas_call(
        functools.partial(edge_kernel, nt, ns),
        out_shape=jax.ShapeDtypeStruct((own, targets), BF16),
        in_specs=[vmem, vmem, vmem, vmem, hbm, hbm, vmem, pl.BlockSpec(memory_space=pltpu.SMEM)],
        out_specs=vmem,
        scratch_shapes=[
            pltpu.VMEM(out_proj.shape, BF16),
            pltpu.VMEM(value_proj.shape, BF16),
            pltpu.VMEM((nt, ns * rows, depth), BF16),
            pltpu.VMEM((nt * sub, depth), BF16),
            pltpu.VMEM((ns * sub, width), BF16),
            pltpu.VMEM((heads, nt * queries, keys), BF16),
            pltpu.VMEM((nt, 1, targets), jnp.int32),
            pltpu.VMEM((groups, total, head_dim), BF16),
            pltpu.VMEM((nt, heads, targets, head_dim), BF16),
            pltpu.VMEM((heads, total, nt * queries), BF16),
            pltpu.VMEM((nt, nt * queries, targets), BF16),
            pltpu.VMEM((nt, total, targets), F32),
            pltpu.VMEM((nt, own, targets), F32),
            pltpu.VMEM((nt, ns, own, targets), BF16),
            pltpu.VMEM((nt, ns, own, targets), BF16),
            pltpu.VMEM((nt, own, targets), BF16),
            pltpu.VMEM((nt, own, targets), BF16),
            pltpu.VMEM((total, 1), jnp.int32),
            sem(3),
            sem(nt), sem(nt), sem(nt), sem(nt), sem(nt), sem(nt),
            sem(nt), sem(nt), sem(nt), sem(nt), sem(nt), sem(nt),
            sem(nt, nx), sem(nt, nx), sem(nt, nx), sem(nt, nx),
            sem(nx), sem(nx), sem(nx), sem(nx),
            sem(nt), sem(nt), sem(nt, ns), sem(nt, ns), sem(nt), sem(nt),
        ],
        compiler_params=pltpu.CompilerParams(
            collective_id=0, has_side_effects=True, vmem_limit_bytes=60 * 1024 * 1024
        ),
    )(
        target_rows, target_pos.reshape(1, targets), decoder_rows, source_pos.reshape(1, total),
        out_proj, value_proj, attention, tile_pattern,
    )


def resident_bytes(nt, ns, width, heads, depth, groups, rows, total, targets):
    weights = heads * depth * 128 + groups * width * 128
    gathered = nt * ns * rows * depth + nt * heads * targets * 128
    return 2 * (weights + gathered) + 4 * nt * total * targets * 2


def shards(
    target_rows, target_pos, decoder_rows, source_pos, out_proj, value_proj, attention, tile_pattern
):
    nt, ns = lax.axis_size("tgt"), lax.axis_size("src")
    heads, depth, head_dim = out_proj.shape
    need = resident_bytes(
        nt, ns, target_rows.shape[1], heads, depth, value_proj.shape[0], target_rows.shape[0],
        source_pos.shape[0], target_pos.shape[0],
    )
    fits = (
        depth % 128 == 0 and head_dim == 128 and ns % 2 == 0 and nt > 2
        and decoder_rows.shape[0] % 16 == 0 and attention.shape[1] % 16 == 0
        and need < 40 * 1024 * 1024
    )
    plan = resident_shards if fits else gathered_shards
    return plan(
        target_rows, target_pos, decoder_rows, source_pos, out_proj, value_proj, attention, tile_pattern
    )


def solution(mesh):
    return jax.shard_map(
        shards,
        mesh=mesh,
        in_specs=(
            P(("grp", "tgt", "src"), None),
            P(("grp", "tgt")),
            P(("grp", "tgt", "src"), None),
            P("grp"),
            P("src", "tgt", None),
            P("src", None, None),
            P(("grp", "src"), "tgt", None),
            P("grp", None),
        ),
        out_specs=P(("grp", "src"), "tgt"),
        check_vma=False,
    )
```

profile of v0, /device:TPU:0, one launch (start us, length us, event | category | flops | bytes accessed | tf_op | source)
XLA Modules:
  0.0 63.5 jit_solution(2825436155714072756)
XLA Ops:
  0.0 62.1 %shard_map.82 = bf16[64,256]{1,0:T(8,128)(2,1)} custom-call(bf16[64,4608]{1,0:T(8,128)(2,1)} %tgt_ref.1, s32[1,256]{1,0:T(1,128)} %bitcast.2, bf16[16,4608]{1,0:T(8,128)(2,1)} %dec_ref.1, s32[1,256]{1,0:T(1,128)} %bitcast.3, bf16[8,1152,128]{2,1,0:T(8,128)(2,1)} %oproj_hbm.1, bf16[4,4608,128]{2,1,0:T(8,128)(2,1)} %vproj_hbm.1, bf16[8,64,256]{2,1,0:T(8,128)(2,1)} %attn_ref.1, ...), custom_call_target="tpu_custom_call" | custom-call | tf_op jit(solution)/shard_map/pallas_call | solution.py:450
  62.1 1.4 %copy.10 = bf16[64,256]{1,0:T(8,128)(2,1)} copy(bf16[64,256]{1,0:T(8,128)(2,1)} %shard_map.82) | data formatting | bytes 65536
where the time goes:
time: 63.7 us; the launch traced here: 63.5 us
  Pallas kernels  62.1 us (97%)
  local copies, waits for them, and re-layouts  1.38 us (2%)
    pallas_call x1, Pallas kernels, resident_shards(): pl.pallas_call(functools.partial(edge_kernel, nt, ns), out_shape=jax.Shap...  62.1 us
    unnamed x1, local copies, waits for them, and re-layouts  1.38 us

commit v1 on v0

v1 whole, which is shorter than its diff:
```python
import functools

import jax
import jax.numpy as jnp
from jax import lax
from jax.experimental import pallas as pl
from jax.experimental.pallas import tpu as pltpu
from jax.sharding import PartitionSpec as P


def passed_along(value, axis, steps):
    count = lax.axis_size(axis)
    pairs = [(source, (source + steps) % count) for source in range(count)]
    return lax.ppermute(value, axis, pairs)


def gathered_shards(
    target_rows, target_pos, decoder_rows, source_pos, out_proj, value_proj, attention, tile_pattern
):
    blocks = lax.axis_size("tgt")
    column = lax.axis_index("tgt")
    src_lane = lax.axis_index("src")
    full_targets, full_sources = (
        lax.all_gather(target_rows, "src", axis=0, tiled=True),
        lax.all_gather(decoder_rows, "src", axis=0, tiled=True),
    )
    tgt_dev = full_targets.shape[0]
    src_dev = full_sources.shape[0]
    sub_rows = decoder_rows.shape[0]
    heads_here = out_proj.shape[0]
    head_dim = out_proj.shape[2]
    groups_here = value_proj.shape[0]
    repeat = heads_here // groups_here
    read_sum = jnp.einsum(
        "td,hde->the",
        full_targets,
        lax.all_gather(out_proj, "tgt", axis=1, tiled=True),
        preferred_element_type=jnp.float32,
    )
    head_reads = read_sum.astype(jnp.bfloat16).reshape(tgt_dev, groups_here, repeat, head_dim)
    values = jnp.einsum("sd,gde->sge", full_sources, value_proj, preferred_element_type=jnp.float32)
    values = values.astype(jnp.bfloat16).reshape(src_dev, groups_here * head_dim)
    attn_table = lax.all_gather(attention, "tgt", axis=1, tiled=True)
    target_attn = jnp.take(attn_table, target_pos, axis=1)
    keyed_attn = jnp.transpose(target_attn, (0, 2, 1))

    def edge_tile(payload, block_index):
        decoder_part, value_part = payload
        key_positions = lax.dynamic_slice_in_dim(source_pos, block_index * src_dev, src_dev)
        weights = jnp.take(keyed_attn, key_positions, axis=1).astype(jnp.float32)
        scores = jnp.einsum(
            "sgd,tgrd->grst",
            value_part.reshape(src_dev, groups_here, head_dim),
            head_reads,
            preferred_element_type=jnp.float32,
        )
        scores = scores.reshape(heads_here, src_dev, tgt_dev)
        mixed_term = jnp.sum(weights * scores, axis=0)
        own_positions = lax.dynamic_slice_in_dim(key_positions, src_lane * sub_rows, sub_rows)
        same_place = (own_positions[:, None] == target_pos[None, :]).astype(jnp.float32)
        direct = (
            jnp.einsum("sd,td->st", decoder_part, full_targets, preferred_element_type=jnp.float32)
            * same_place
        )
        own_rows = lax.dynamic_slice_in_dim(mixed_term, src_lane * sub_rows, sub_rows, 0)
        return lax.dynamic_update_slice_in_dim(
            mixed_term, own_rows + direct, src_lane * sub_rows, 0
        )

    def place_tile(partial_value, payload, block_index):
        kept_flag = tile_pattern[block_index, column]
        piece_tile = edge_tile(payload, block_index) * kept_flag.astype(jnp.float32)
        return lax.dynamic_update_slice_in_dim(partial_value, piece_tile, block_index * src_dev, 0)

    own_block = (decoder_rows, values)
    partial_value = jnp.zeros((blocks * src_dev, tgt_dev), jnp.float32)
    partial_value = place_tile(partial_value, own_block, column)

    def cycle_turn(turn_index, state_carry):
        forward_block, backward_block, running = state_carry
        forward_block = passed_along((forward_block[0], forward_block[1]), "tgt", 1)
        backward_block = passed_along((backward_block[0], backward_block[1]), "tgt", -1)
        running = place_tile(running, forward_block, (column - turn_index) % blocks)
        running = place_tile(running, backward_block, (column + turn_index) % blocks)
        return (forward_block, backward_block, running)

    forward_block, backward_block, partial_value = lax.fori_loop(
        1, blocks // 2, cycle_turn, (own_block, own_block, partial_value)
    )
    forward_block = passed_along((forward_block[0], forward_block[1]), "tgt", 1)
    partial_value = place_tile(partial_value, forward_block, (column - blocks // 2) % blocks)
    summed = lax.psum_scatter(partial_value, "src", scatter_dimension=0, tiled=True)
    return summed.astype(jnp.bfloat16)


F32 = jnp.float32
BF16 = jnp.bfloat16
MESH = pl.DeviceIdType.MESH


def dot(a, b):
    return jnp.dot(a, b, preferred_element_type=F32)


def dot_nt(a, b):
    return lax.dot_general(a, b, (((1,), (1,)), ((), ())), preferred_element_type=F32)


def edge_kernel(
    nt, ns, tgt_hbm, tpos_hbm, dec_hbm, srow_hbm, oproj_hbm, vproj_hbm, attn_hbm, pat_ref,
    out_ref,
    oproj, vproj, tslices, dslices, decfull, attn, tpos, srow, values, reads, pick, attn_n, onehot,
    edges, core_in, x_out, x_in, z_out, z_in, scol_ref,
    local_sem, zt_s, zt_r, zd_s, zd_r, zp_s, zp_r, ar_s, al_s, a_r, vr_s, vl_s, v_r,
    xt_s, xt_r, ct_s, ct_r, xf_s, xf_r, cf_s, cf_r, ce_s, ce_r, xe_s, xe_r, ze_s, ze_r,
):
    c = lax.axis_index("tgt")
    s = lax.axis_index("src")
    nx = ns // 2
    x = s // 2
    core = s % 2
    mate = x * 2 + 1 - core
    rows, depth = tslices.shape[1] // ns, tslices.shape[2]
    sub = dec_hbm.shape[0]
    heads = oproj.shape[0]
    groups = vproj.shape[0]
    repeat = heads // groups
    block = sub * ns
    queries, keys = attn_hbm.shape[1:]
    targets = tpos.shape[2]
    total = scol_ref.shape[0]
    own = edges.shape[1] // ns
    hd = vproj.shape[2]

    inner = (c > 0) & (c + 1 < nt)

    def table(rank):
        rows_of = [[i] + sorted((b for b in range(nt) if b != i), key=lambda b: rank(i, b)) for i in range(nt)]

        def entry(j):
            b = rows_of[0][j]
            for i in range(1, nt):
                b = jnp.where(c == i, rows_of[i][j], b)
            return b

        return [entry(j) for j in range(nt)]

    def sent_rank(i, b):
        return abs(b - i) if 0 < i < nt - 1 else -abs(b - i)

    def got_rank(i, b):
        far = abs(b - i)
        return (-far, b in (0, nt - 1)) if 0 < i < nt - 1 else (b in (0, nt - 1) and -far, far)

    targets_of = table(sent_rank)
    order = table(got_rank)
    last_of = table(lambda i, b: -b)

    def xsrc(dx):
        return lax.rem(x + dx, nx) * 2 + core

    pending = []

    def remote(src, dst, ssem, rsem, axis, index):
        return pltpu.make_async_remote_copy(
            src_ref=src, dst_ref=dst, send_sem=ssem, recv_sem=rsem,
            device_id={axis: index}, device_id_type=MESH,
        )

    def send(src, dst, ssem, rsem, axis, index):
        remote(src, dst, ssem, rsem, axis, index).start()
        pending.append((None, lambda: remote(src, dst, ssem, rsem, axis, index)))

    def arrived(dst, rsem):
        remote(dst, dst, local_sem.at[0], rsem, "src", mate).wait_recv()

    barrier = pltpu.get_barrier_semaphore()
    for j in range(1, nt):
        pl.semaphore_signal(barrier, inc=1, device_id={"tgt": order[j]}, device_id_type=MESH)
    for dx in range(1, nx):
        pl.semaphore_signal(barrier, inc=1, device_id={"src": xsrc(dx)}, device_id_type=MESH)
    pl.semaphore_signal(barrier, inc=1, device_id={"src": mate}, device_id_type=MESH)

    def cols(b):
        return pl.ds(pl.multiple_of(b * depth, 128), depth)

    def trow(lane):
        return pl.ds(pl.multiple_of(lane * rows, rows), rows)

    def drow(lane):
        return pl.ds(pl.multiple_of(lane * sub, sub), sub)

    def qrow(b):
        return pl.ds(pl.multiple_of(b * queries, queries), queries)

    def vrow(b):
        return pl.ds(pl.multiple_of(b * block, block), block)

    def erow(lane):
        return pl.ds(pl.multiple_of(lane * own, own), own)

    fetch = [
        pltpu.make_async_copy(dec_hbm, decfull.at[drow(s)], local_sem.at[1]),
        pltpu.make_async_copy(srow_hbm, srow, local_sem.at[2]),
        pltpu.make_async_copy(tpos_hbm, tpos.at[c], local_sem.at[3]),
        pltpu.make_async_copy(vproj_hbm, vproj, local_sem.at[4]),
        pltpu.make_async_copy(tgt_hbm.at[:, cols(c)], tslices.at[c, trow(s)], local_sem.at[5]),
        pltpu.make_async_copy(dec_hbm.at[:, cols(c)], dslices.at[drow(c)], local_sem.at[6]),
        pltpu.make_async_copy(oproj_hbm, oproj, local_sem.at[7]),
        pltpu.make_async_copy(attn_hbm, attn.at[:, qrow(c), :], local_sem.at[8]),
    ]
    for cp in fetch[:7]:
        cp.start()
    pl.semaphore_wait(barrier, nt - 1 + nx)

    half = keys // 2
    lowest = half // queries if half % 128 == 0 else 0

    def attn_copy(b, g, ssem, device, act, src=None):
        part = pl.ds(g * repeat, repeat)

        def view(lanes):
            dst = attn.at[part, qrow(b), lanes]
            return dst if src is None else src.at[part, :, lanes], dst

        @pl.when(b < lowest)
        def _():
            a, d = view(pl.ds(0, half))
            act(remote(a, d, ssem.at[b, g], a_r.at[b, g], "tgt", device))

        @pl.when(b >= lowest)
        def _():
            a, d = view(pl.ds(0, keys))
            act(remote(a, d, ssem.at[b, g], a_r.at[b, g], "tgt", device))

    def value_copy(b, ssem, device):
        dst = values.at[:, vrow(b), :]
        return remote(dst, dst, ssem.at[b], v_r.at[b], "tgt", device)

    start = lambda copy: copy.start()
    wait_send = lambda copy: copy.wait_send()
    wait_recv = lambda copy: copy.wait_recv()

    def rightward(act):
        pl.when(c + 1 < nt)(act)

    def leftward(act):
        pl.when(c > 0)(act)

    for dx in range(1, nx):
        send(dec_hbm, decfull.at[drow(s)], xf_s.at[dx], xf_r.at[x], "src", xsrc(dx))
    send(dec_hbm, decfull.at[drow(s)], cf_s.at[x], cf_r.at[x], "src", mate)
    def spread_copies(b):
        return (
            remote(tgt_hbm.at[:, cols(b)], tslices.at[c, trow(s)], zt_s.at[b], zt_r.at[c], "tgt", b),
            remote(dec_hbm.at[:, cols(b)], dslices.at[drow(c)], zd_s.at[b], zd_r.at[c], "tgt", b),
            remote(tpos_hbm, tpos.at[c], zp_s.at[b], zp_r.at[c], "tgt", b),
        )

    def spread(j):
        b = targets_of[j]
        for copy in spread_copies(b):
            copy.start()

    spread(1)
    spread(2)
    for dx in range(1, nx):
        send(tgt_hbm.at[:, cols(c)], tslices.at[c, trow(s)], xt_s.at[c, dx], xt_r.at[c, x], "src", xsrc(dx))
    send(tgt_hbm.at[:, cols(c)], tslices.at[c, trow(s)], ct_s.at[c, x], ct_r.at[c, x], "src", mate)

    fetch[1].wait()
    fetch[2].wait()
    scol_ref[...] = jnp.transpose(jnp.broadcast_to(srow[...], (128, total)))[:, :1]
    pick[...] = (scol_ref[...] == lax.broadcasted_iota(jnp.int32, (total, keys), 1)).astype(BF16)
    for b in range(lowest):
        attn[:, b * queries:(b + 1) * queries, half:] = jnp.zeros((heads, queries, keys - half), BF16)
    fetch[7].start()

    def relay(k, copy_in, copy_on):
        @pl.when(c - k >= 0)
        def _():
            copy_in(c - k)
            rightward(lambda: copy_on(c - k, 0))

        @pl.when(c + k < nt)
        def _():
            copy_in(c + k)
            leftward(lambda: copy_on(c + k, 1))

    def attn_step(k, g):
        relay(
            k, lambda b: attn_copy(b, g, ar_s, c, wait_recv),
            lambda b, left: attn_copy(b, g, al_s if left else ar_s, c - 1 if left else c + 1, start),
        )

    def value_step(k):
        relay(
            k, lambda b: value_copy(b, vr_s, c).wait_recv(),
            lambda b, left: value_copy(b, vl_s if left else vr_s, c - 1 if left else c + 1).start(),
        )

    def take(j):
        b = order[j]
        arrived(tslices.at[b, trow(s)], zt_r.at[b])
        for dx in range(1, nx):
            send(tslices.at[b, trow(s)], tslices.at[b, trow(s)], xt_s.at[b, dx], xt_r.at[b, x], "src", xsrc(dx))
        send(tslices.at[b, trow(s)], tslices.at[b, trow(s)], ct_s.at[b, x], ct_r.at[b, x], "src", mate)

    fetch[0].wait()
    for dx in range(1, nx):
        z = lax.rem(x + dx, nx)
        y = xsrc(dx)
        arrived(decfull.at[drow(y)], xf_r.at[z])
        send(decfull.at[drow(y)], decfull.at[drow(y)], cf_s.at[z], cf_r.at[z], "src", mate)
    for dx in range(nx):
        z = lax.rem(x + dx, nx)
        arrived(decfull.at[drow(z * 2 + 1 - core)], cf_r.at[z])
    fetch[3].wait()

    @pl.loop(0, groups)
    def _(g):
        values[g, vrow(c)] = dot(decfull[...], vproj[g]).astype(BF16)

    fetch[7].wait()
    rightward(lambda: value_copy(c, vr_s, c + 1).start())
    leftward(lambda: value_copy(c, vl_s, c - 1).start())
    for j in range(3, nt):
        spread(j)
    rightward(lambda: attn_copy(c, 0, ar_s, c + 1, start, attn_hbm))
    leftward(lambda: attn_copy(c, 0, al_s, c - 1, start, attn_hbm))
    rightward(lambda: attn_copy(c, 1, ar_s, c + 1, start, attn_hbm))
    leftward(lambda: attn_copy(c, 1, al_s, c - 1, start, attn_hbm))
    rightward(lambda: attn_copy(c, 2, ar_s, c + 1, start, attn_hbm))
    leftward(lambda: attn_copy(c, 2, al_s, c - 1, start, attn_hbm))
    rightward(lambda: attn_copy(c, 3, ar_s, c + 1, start, attn_hbm))
    leftward(lambda: attn_copy(c, 3, al_s, c - 1, start, attn_hbm))

    def cross(j):
        b = order[j]
        for dx in range(1, nx):
            z = lax.rem(x + dx, nx)
            y = z * 2 + core
            arrived(tslices.at[b, trow(y)], xt_r.at[b, z])
            send(tslices.at[b, trow(y)], tslices.at[b, trow(y)], ct_s.at[b, z], ct_r.at[b, z], "src", mate)

    def ready(j):
        b = order[j]
        if j == 0:
            fetch[4].wait()
            fetch[5].wait()
            fetch[6].wait()
        else:
            arrived(dslices.at[drow(b)], zd_r.at[b])
            arrived(tpos.at[b], zp_r.at[b])
        for dx in range(nx):
            z = lax.rem(x + dx, nx)
            arrived(tslices.at[b, trow(z * 2 + 1 - core)], ct_r.at[b, z])

    def read_block(j):
        b = order[j]

        @pl.loop(0, groups)
        def _(g):
            pair = jnp.concatenate([oproj[g * repeat + r] for r in range(repeat)], axis=1)
            reads[b, g] = dot(tslices[b], pair).astype(BF16)
        onehot[b] = (
            lax.broadcasted_iota(jnp.int32, (nt * queries, targets), 0) == tpos[b]
        ).astype(BF16)

    def start_edges(j):
        b = order[j]
        direct = dot_nt(dslices[...], tslices[b])
        here = tpos[b]
        edges[b] = jnp.zeros(edges.shape[1:], F32)
        for p in range(nt):
            at = pl.ds(pl.multiple_of(p * block + s * sub, sub), sub)
            same = (scol_ref[at] == here).astype(F32)
            edges[b, at] = direct[p * sub:(p + 1) * sub] * same

    def pick_keys(g):
        for r in range(repeat):
            attn_n[g * repeat + r] = dot_nt(pick[...], attn[g * repeat + r]).astype(BF16)

    def mix(g, b):
        terms = None
        for r in range(repeat):
            term = dot(attn_n[g * repeat + r], onehot[b]) * dot_nt(values[g], reads[b, g, :, r * hd:(r + 1) * hd])
            terms = term if terms is None else terms + term
        edges[b] += terms

    def to_mate(b):
        for z in range(nx):
            send(edges.at[b, erow(z * 2 + 1 - core)], core_in.at[b, z], ce_s.at[b, z], ce_r.at[b, z], "src", mate)

    def over_x(b):
        for dx in range(1, nx):
            z = lax.rem(x + dx, nx)
            arrived(core_in.at[b, z], ce_r.at[b, z])
            x_out[b, z] = (edges[b, erow(z * 2 + core)] + core_in[b, z]).astype(BF16)
            send(x_out.at[b, z], x_in.at[b, x], xe_s.at[b, z], xe_r.at[b, x], "src", z * 2 + core)
        arrived(core_in.at[b, x], ce_r.at[b, x])

    def over_z(b, away):
        mine = edges[b, erow(s)] + core_in[b, x]
        for dx in range(1, nx):
            z = lax.rem(x + dx, nx)
            arrived(x_in.at[b, z], xe_r.at[b, z])
            mine += x_in[b, z].astype(F32)
        if away:
            z_out[b] = mine.astype(BF16)
            send(z_out.at[b], z_in.at[c], ze_s.at[b], ze_r.at[c], "tgt", b)
        return mine

    take(1)
    cross(0)
    ready(0)
    read_block(0)
    take(2)
    cross(1)
    take(3)
    value_step(1)
    ready(1)
    read_block(1)
    cross(2)
    attn_step(1, 0)
    ready(2)
    read_block(2)
    attn_step(1, 1)
    cross(3)
    attn_step(1, 2)
    ready(3)
    read_block(3)
    attn_step(1, 3)
    start_edges(0)
    value_step(2)
    attn_step(2, 0)
    start_edges(1)
    start_edges(2)
    start_edges(3)
    value_step(3)
    for g in range(groups):
        for k in range(1, nt):
            if (k, g) not in [(1, 0), (1, 1), (1, 2), (1, 3), (2, 0)]:
                attn_step(k, g)
        pick_keys(g)
        for j in list(range(1, nt)) + [0]:
            mix(g, last_of[j])
            if g == groups - 1:
                to_mate(last_of[j])
    for j in list(range(1, nt)) + [0]:
        over_x(last_of[j])
    for j in range(1, nt):
        over_z(last_of[j], True)
    mine = over_z(c, False)
    for j in range(1, nt):
        for copy in spread_copies(order[j]):
            copy.wait_send()
    for _, again in pending:
        again().wait_send()
    for k in range(nt):
        @pl.when((c - k >= 0) & (c + 1 < nt))
        def _():
            for g in range(groups):
                attn_copy(c - k, g, ar_s, c + 1, wait_send)
            value_copy(c - k, vr_s, c + 1).wait_send()

        @pl.when((c + k < nt) & (c > 0))
        def _():
            for g in range(groups):
                attn_copy(c + k, g, al_s, c - 1, wait_send)
            value_copy(c + k, vl_s, c - 1).wait_send()

    for j in range(1, nt):
        b = order[j]
        arrived(z_in.at[b], ze_r.at[b])
        mine += z_in[b].astype(F32)
    kept = pat_ref[(s * own) // block, c]
    out_ref[...] = (mine * kept.astype(F32)).astype(BF16)


def resident_shards(
    target_rows, target_pos, decoder_rows, source_pos, out_proj, value_proj, attention, tile_pattern
):
    nt, ns = lax.axis_size("tgt"), lax.axis_size("src")
    rows = target_rows.shape[0]
    sub, width = decoder_rows.shape
    heads, depth, head_dim = out_proj.shape
    groups = value_proj.shape[0]
    repeat = heads // groups
    _, queries, keys = attention.shape
    total = source_pos.shape[0]
    targets = target_pos.shape[0]
    own = total // ns
    nx = ns // 2
    vmem = pl.BlockSpec(memory_space=pltpu.VMEM)
    hbm = pl.BlockSpec(memory_space=pl.ANY)
    sem = lambda *shape: pltpu.SemaphoreType.DMA(shape)
    return pl.pallas_call(
        functools.partial(edge_kernel, nt, ns),
        out_shape=jax.ShapeDtypeStruct((own, targets), BF16),
        in_specs=[hbm, hbm, hbm, hbm, hbm, hbm, hbm, pl.BlockSpec(memory_space=pltpu.SMEM)],
        out_specs=vmem,
        scratch_shapes=[
            pltpu.VMEM(out_proj.shape, BF16),
            pltpu.VMEM(value_proj.shape, BF16),
            pltpu.VMEM((nt, ns * rows, depth), BF16),
            pltpu.VMEM((nt * sub, depth), BF16),
            pltpu.VMEM((ns * sub, width), BF16),
            pltpu.VMEM((heads, nt * queries, keys), BF16),
            pltpu.VMEM((nt, 1, targets), jnp.int32),
            pltpu.VMEM((1, total), jnp.int32),
            pltpu.VMEM((groups, total, head_dim), BF16),
            pltpu.VMEM((nt, groups, targets, repeat * head_dim), BF16),
            pltpu.VMEM((total, keys), BF16),
            pltpu.VMEM((heads, total, nt * queries), BF16),
            pltpu.VMEM((nt, nt * queries, targets), BF16),
            pltpu.VMEM((nt, total, targets), F32),
            pltpu.VMEM((nt, nx, own, targets), F32),
            pltpu.VMEM((nt, nx, own, targets), BF16),
            pltpu.VMEM((nt, nx, own, targets), BF16),
            pltpu.VMEM((nt, own, targets), BF16),
            pltpu.VMEM((nt, own, targets), BF16),
            pltpu.VMEM((total, 1), jnp.int32),
            sem(9),
            sem(nt), sem(nt), sem(nt), sem(nt), sem(nt), sem(nt),
            sem(nt, groups), sem(nt, groups), sem(nt, groups), sem(nt), sem(nt), sem(nt),
            sem(nt, nx), sem(nt, nx), sem(nt, nx), sem(nt, nx),
            sem(nx), sem(nx), sem(nx), sem(nx),
            sem(nt, nx), sem(nt, nx), sem(nt, nx), sem(nt, nx), sem(nt), sem(nt),
        ],
        compiler_params=pltpu.CompilerParams(
            collective_id=0, has_side_effects=True, vmem_limit_bytes=60 * 1024 * 1024
        ),
    )(
        target_rows, target_pos.reshape(1, targets), decoder_rows, source_pos.reshape(1, total),
        out_proj, value_proj, attention, tile_pattern,
    )


def resident_bytes(nt, ns, width, heads, depth, groups, rows, total, targets):
    weights = heads * depth * 128 + groups * width * 128
    gathered = nt * ns * rows * depth + nt * heads * targets * 128
    return 2 * (weights + gathered) + 4 * nt * total * targets * 2


def shards(
    target_rows, target_pos, decoder_rows, source_pos, out_proj, value_proj, attention, tile_pattern
):
    nt, ns = lax.axis_size("tgt"), lax.axis_size("src")
    heads, depth, head_dim = out_proj.shape
    need = resident_bytes(
        nt, ns, target_rows.shape[1], heads, depth, value_proj.shape[0], target_rows.shape[0],
        source_pos.shape[0], target_pos.shape[0],
    )
    fits = (
        depth % 128 == 0 and head_dim == 128 and ns % 2 == 0 and nt > 2
        and decoder_rows.shape[0] % 16 == 0 and attention.shape[1] % 16 == 0
        and need < 40 * 1024 * 1024
    )
    plan = resident_shards if fits else gathered_shards
    return plan(
        target_rows, target_pos, decoder_rows, source_pos, out_proj, value_proj, attention, tile_pattern
    )


def solution(mesh):
    return jax.shard_map(
        shards,
        mesh=mesh,
        in_specs=(
            P(("grp", "tgt", "src"), None),
            P(("grp", "tgt")),
            P(("grp", "tgt", "src"), None),
            P("grp"),
            P("src", "tgt", None),
            P("src", None, None),
            P(("grp", "src"), "tgt", None),
            P("grp", None),
        ),
        out_specs=P(("grp", "src"), "tgt"),
        check_vma=False,
    )
```

time: 63.7 us -> 52.4 us (0.82)
  Pallas kernels: 62.1 us -> 50.8 us
    pallas_call x1, Pallas kernels: 62.1 us -> 50.8 us  [resident_shards(): pl.pallas_call(functools.partial(edge_kernel, nt, ns), out_shape=jax.Shap...]
where the time goes in v1:
time: 52.4 us; the launch traced here: 52.2 us
  Pallas kernels  50.8 us (97%)
  local copies, waits for them, and re-layouts  1.38 us (3%)
    pallas_call x1, Pallas kernels, resident_shards(): pl.pallas_call(functools.partial(edge_kernel, nt, ns), out_shape=jax.Shap...  50.8 us
    unnamed x1, local copies, waits for them, and re-layouts  1.38 us

profile of v1, /device:TPU:0, one launch (start us, length us, event | category | flops | bytes accessed | tf_op | source)
XLA Modules:
  0.0 52.2 jit_solution(3608123995481073094)
XLA Ops:
  0.0 50.8 %shard_map.82 = bf16[64,256]{1,0:T(8,128)(2,1)} custom-call(bf16[64,4608]{1,0:T(8,128)(2,1)} %tgt_hbm.1, s32[1,256]{1,0:T(1,128)} %bitcast.2, bf16[16,4608]{1,0:T(8,128)(2,1)} %dec_hbm.1, s32[1,256]{1,0:T(1,128)} %bitcast.3, bf16[8,1152,128]{2,1,0:T(8,128)(2,1)} %oproj_hbm.1, bf16[4,4608,128]{2,1,0:T(8,128)(2,1)} %vproj_hbm.1, bf16[8,64,256]{2,1,0:T(8,128)(2,1)} %attn_hbm.1, ...), custom_call_target="tpu_custom_call" | custom-call | tf_op jit(solution)/shard_map/pallas_call | solution.py:498
  50.8 1.4 %copy.10 = bf16[64,256]{1,0:T(8,128)(2,1)} copy(bf16[64,256]{1,0:T(8,128)(2,1)} %shard_map.82) | data formatting | bytes 65536

commit v2 on v1

--- a/solution.py
+++ b/solution.py
@@ -107,10 +107,10 @@
 
 
 def edge_kernel(
-    nt, ns, tgt_hbm, tpos_hbm, dec_hbm, srow_hbm, oproj_hbm, vproj_hbm, attn_hbm, pat_ref,
+    nt, ns, tgt_hbm, tpos_hbm, dec_hbm, srow_hbm, oproj_hbm, vproj_hbm, attn_hbm, pat_hbm,
     out_ref,
-    oproj, vproj, tslices, dslices, decfull, attn, tpos, srow, values, reads, pick, attn_n, onehot,
-    edges, core_in, x_out, x_in, z_out, z_in, scol_ref,
+    oproj, vproj, tslices, dslices, decfull, attn, packs, tpos, srow, values, reads, pick, attn_n, onehot,
+    edges, core_in, x_out, x_in, z_out, z_in, scol_ref, pat_ref,
     local_sem, zt_s, zt_r, zd_s, zd_r, zp_s, zp_r, ar_s, al_s, a_r, vr_s, vl_s, v_r,
     xt_s, xt_r, ct_s, ct_r, xf_s, xf_r, cf_s, cf_r, ce_s, ce_r, xe_s, xe_r, ze_s, ze_r,
 ):
@@ -208,16 +208,22 @@
         pltpu.make_async_copy(dec_hbm.at[:, cols(c)], dslices.at[drow(c)], local_sem.at[6]),
         pltpu.make_async_copy(oproj_hbm, oproj, local_sem.at[7]),
         pltpu.make_async_copy(attn_hbm, attn.at[:, qrow(c), :], local_sem.at[8]),
+        pltpu.make_async_copy(pat_hbm, pat_ref, local_sem.at[9]),
     ]
-    for cp in fetch[:7]:
+    for cp in fetch[:7] + fetch[8:]:
         cp.start()
     pl.semaphore_wait(barrier, nt - 1 + nx)
 
+    chunks = [(g * repeat, repeat) for g in range(groups - 1)]
+    chunks += [(heads - repeat + r, 1) for r in range(repeat)]
     half = keys // 2
     lowest = half // queries if half % 128 == 0 else 0
+    packed = nt - 2
+    if repeat != 2 or packed < lowest or lowest == 0 or (packed + 1) * queries - half != half // 2:
+        packed = -1
 
     def attn_copy(b, g, ssem, device, act, src=None):
-        part = pl.ds(g * repeat, repeat)
+        part = pl.ds(*chunks[g])
 
         def view(lanes):
             dst = attn.at[part, qrow(b), lanes]
@@ -228,7 +234,12 @@
             a, d = view(pl.ds(0, half))
             act(remote(a, d, ssem.at[b, g], a_r.at[b, g], "tgt", device))
 
-        @pl.when(b >= lowest)
+        if packed >= 0 and g < groups:
+            @pl.when(b == packed)
+            def _():
+                act(remote(packs.at[g], packs.at[g], ssem.at[b, g], a_r.at[b, g], "tgt", device))
+
+        @pl.when((b >= lowest) & (b != packed))
         def _():
             a, d = view(pl.ds(0, keys))
             act(remote(a, d, ssem.at[b, g], a_r.at[b, g], "tgt", device))
@@ -253,9 +264,15 @@
     def spread_copies(b):
         return (
             remote(tgt_hbm.at[:, cols(b)], tslices.at[c, trow(s)], zt_s.at[b], zt_r.at[c], "tgt", b),
-            remote(dec_hbm.at[:, cols(b)], dslices.at[drow(c)], zd_s.at[b], zd_r.at[c], "tgt", b),
             remote(tpos_hbm, tpos.at[c], zp_s.at[b], zp_r.at[c], "tgt", b),
         )
+
+    def slice_copy(b):
+        return remote(dec_hbm.at[:, cols(b)], dslices.at[drow(c)], zd_s.at[b], zd_r.at[c], "tgt", b)
+
+    def send_slices():
+        for j in range(1, nt):
+            slice_copy(targets_of[j]).start()
 
     def spread(j):
         b = targets_of[j]
@@ -322,18 +339,18 @@
         values[g, vrow(c)] = dot(decfull[...], vproj[g]).astype(BF16)
 
     fetch[7].wait()
+    if packed >= 0:
+        @pl.when(c == packed)
+        def _():
+            at = slice(packed * queries, (packed + 1) * queries)
+            for g in range(groups):
+                packs[g, 0] = attn[2 * g, at, :half]
+                packs[g, 1] = attn[2 * g + 1, at, :half]
+                packs[g, 2] = jnp.concatenate(
+                    [attn[2 * g + r, at, half:half + half // 2] for r in range(2)], axis=1
+                )
     rightward(lambda: value_copy(c, vr_s, c + 1).start())
     leftward(lambda: value_copy(c, vl_s, c - 1).start())
-    for j in range(3, nt):
-        spread(j)
-    rightward(lambda: attn_copy(c, 0, ar_s, c + 1, start, attn_hbm))
-    leftward(lambda: attn_copy(c, 0, al_s, c - 1, start, attn_hbm))
-    rightward(lambda: attn_copy(c, 1, ar_s, c + 1, start, attn_hbm))
-    leftward(lambda: attn_copy(c, 1, al_s, c - 1, start, attn_hbm))
-    rightward(lambda: attn_copy(c, 2, ar_s, c + 1, start, attn_hbm))
-    leftward(lambda: attn_copy(c, 2, al_s, c - 1, start, attn_hbm))
-    rightward(lambda: attn_copy(c, 3, ar_s, c + 1, start, attn_hbm))
-    leftward(lambda: attn_copy(c, 3, al_s, c - 1, start, attn_hbm))
 
     def cross(j):
         b = order[j]
@@ -347,46 +364,74 @@
         b = order[j]
         if j == 0:
             fetch[4].wait()
-            fetch[5].wait()
             fetch[6].wait()
         else:
-            arrived(dslices.at[drow(b)], zd_r.at[b])
             arrived(tpos.at[b], zp_r.at[b])
         for dx in range(nx):
             z = lax.rem(x + dx, nx)
             arrived(tslices.at[b, trow(z * 2 + 1 - core)], ct_r.at[b, z])
 
-    def read_block(j):
+    def read_block(j, part):
         b = order[j]
-
-        @pl.loop(0, groups)
+        share = groups // 2
+
+        @pl.loop(part * share, groups if part else share)
         def _(g):
             pair = jnp.concatenate([oproj[g * repeat + r] for r in range(repeat)], axis=1)
             reads[b, g] = dot(tslices[b], pair).astype(BF16)
-        onehot[b] = (
-            lax.broadcasted_iota(jnp.int32, (nt * queries, targets), 0) == tpos[b]
-        ).astype(BF16)
-
-    def start_edges(j):
-        b = order[j]
+
+        if part:
+            onehot[b] = (
+                lax.broadcasted_iota(jnp.int32, (nt * queries, targets), 0) == tpos[b]
+            ).astype(BF16)
+
+    def wait_slices():
+        fetch[5].wait()
+        for j in range(1, nt):
+            arrived(dslices.at[drow(order[j])], zd_r.at[order[j]])
+
+    def add_direct(b):
         direct = dot_nt(dslices[...], tslices[b])
         here = tpos[b]
-        edges[b] = jnp.zeros(edges.shape[1:], F32)
         for p in range(nt):
             at = pl.ds(pl.multiple_of(p * block + s * sub, sub), sub)
             same = (scol_ref[at] == here).astype(F32)
-            edges[b, at] = direct[p * sub:(p + 1) * sub] * same
-
-    def pick_keys(g):
-        for r in range(repeat):
-            attn_n[g * repeat + r] = dot_nt(pick[...], attn[g * repeat + r]).astype(BF16)
-
-    def mix(g, b):
+            edges[b, at] += direct[p * sub:(p + 1) * sub] * same
+
+    def unpack(g):
+        at = slice(packed * queries, (packed + 1) * queries)
+        both = packs[g, 2].astype(F32)
+        lane = lax.broadcasted_iota(jnp.int32, both.shape, 1)
+        for r in range(2):
+            attn[2 * g + r, at, :half] = packs[g, r]
+            upper = pltpu.roll(both, half // 2, 1) if r else both
+            attn[2 * g + r, at, half:] = jnp.where(lane < half // 2, upper, 0.0).astype(BF16)
+
+    def pick_keys(i):
+        if packed >= 0 and i < groups:
+            pl.when(c != packed)(lambda: unpack(i))
+        for h in range(chunks[i][0], sum(chunks[i])):
+            attn_n[h] = dot_nt(pick[...], attn[h]).astype(BF16)
+
+    def issue(g):
+        rightward(lambda: attn_copy(c, g, ar_s, c + 1, start, attn_hbm))
+        leftward(lambda: attn_copy(c, g, al_s, c - 1, start, attn_hbm))
+
+    def mix_all(g):
+        for j in range(nt):
+            mix(g, last_of[j])
+
+    def add_all():
+        for j in range(nt):
+            add_direct(last_of[j])
+
+    def mix(i, b):
         terms = None
-        for r in range(repeat):
-            term = dot(attn_n[g * repeat + r], onehot[b]) * dot_nt(values[g], reads[b, g, :, r * hd:(r + 1) * hd])
+        for h in range(chunks[i][0], sum(chunks[i])):
+            g, r = h // repeat, h % repeat
+            term = dot(attn_n[h], onehot[b]) * dot_nt(values[g], reads[b, g, :, r * hd:(r + 1) * hd])
             terms = term if terms is None else terms + term
-        edges[b] += terms
+        edges[b] = terms if i == 0 else edges[b] + terms
 
     def to_mate(b):
         for z in range(nx):
@@ -411,62 +456,94 @@
             send(z_out.at[b], z_in.at[c], ze_s.at[b], ze_r.at[c], "tgt", b)
         return mine
 
+    spread(3)
+    issue(0)
     take(1)
+    issue(1)
+    take(2)
     cross(0)
+    issue(2)
+    cross(1)
+    value_step(1)
     ready(0)
-    read_block(0)
-    take(2)
-    cross(1)
     take(3)
-    value_step(1)
+    issue(3)
+    read_block(0, 1)
     ready(1)
-    read_block(1)
+    read_block(1, 0)
+    attn_step(1, 0)
+    issue(4)
+    read_block(0, 0)
+    attn_step(1, 1)
+    read_block(1, 1)
+    attn_step(1, 2)
+    value_step(2)
+    attn_step(1, 3)
     cross(2)
-    attn_step(1, 0)
     ready(2)
-    read_block(2)
-    attn_step(1, 1)
+    attn_step(2, 0)
+    read_block(2, 1)
+    send_slices()
     cross(3)
-    attn_step(1, 2)
+    value_step(3)
+    attn_step(2, 1)
+    read_block(2, 0)
     ready(3)
-    read_block(3)
-    attn_step(1, 3)
-    start_edges(0)
-    value_step(2)
-    attn_step(2, 0)
-    start_edges(1)
-    start_edges(2)
-    start_edges(3)
-    value_step(3)
-    for g in range(groups):
-        for k in range(1, nt):
-            if (k, g) not in [(1, 0), (1, 1), (1, 2), (1, 3), (2, 0)]:
-                attn_step(k, g)
-        pick_keys(g)
-        for j in list(range(1, nt)) + [0]:
-            mix(g, last_of[j])
-            if g == groups - 1:
-                to_mate(last_of[j])
-    for j in list(range(1, nt)) + [0]:
-        over_x(last_of[j])
+    read_block(3, 1)
+    attn_step(3, 0)
+    pick_keys(0)
+    read_block(3, 0)
+    attn_step(1, 4)
+    mix_all(0)
+    attn_step(2, 2)
+    attn_step(3, 1)
+    pick_keys(1)
+    attn_step(2, 3)
+    mix_all(1)
+    wait_slices()
+    add_all()
+    attn_step(3, 2)
+    pick_keys(2)
+    mix_all(2)
+    attn_step(2, 4)
+    attn_step(3, 3)
+    pick_keys(3)
+    mix_all(3)
+    attn_step(3, 4)
+    last = len(chunks) - 1
+    pick_keys(last)
+    mix(last, last_of[1])
+    to_mate(last_of[1])
+    mix(last, last_of[2])
+    to_mate(last_of[2])
+    for j in range(3, nt):
+        mix(last, last_of[j])
+        to_mate(last_of[j])
+        over_x(last_of[j - 2])
+    mix(last, c)
+    to_mate(c)
+    over_x(last_of[nt - 2])
+    over_x(last_of[nt - 1])
+    over_x(c)
     for j in range(1, nt):
         over_z(last_of[j], True)
     mine = over_z(c, False)
+    fetch[8].wait()
     for j in range(1, nt):
-        for copy in spread_copies(order[j]):
+        for copy in spread_copies(order[j]) + (slice_copy(order[j]),):
             copy.wait_send()
     for _, again in pending:
         again().wait_send()
     for k in range(nt):
         @pl.when((c - k >= 0) & (c + 1 < nt))
         def _():
-            for g in range(groups):
+            for g in range(len(chunks)):
                 attn_copy(c - k, g, ar_s, c + 1, wait_send)
             value_copy(c - k, vr_s, c + 1).wait_send()
 
         @pl.when((c + k < nt) & (c > 0))
         def _():
-            for g in range(groups):
+            for g in range(len(chunks)):
                 attn_copy(c + k, g, al_s, c - 1, wait_send)
             value_copy(c + k, vl_s, c - 1).wait_send()
 
@@ -497,8 +574,8 @@
     sem = lambda *shape: pltpu.SemaphoreType.DMA(shape)
     return pl.pallas_call(
         functools.partial(edge_kernel, nt, ns),
-        out_shape=jax.ShapeDtypeStruct((own, targets), BF16),
-        in_specs=[hbm, hbm, hbm, hbm, hbm, hbm, hbm, pl.BlockSpec(memory_space=pltpu.SMEM)],
+        out_shape=pltpu.VMEM((own, targets), BF16),
+        in_specs=[hbm] * 8,
         out_specs=vmem,
         scratch_shapes=[
             pltpu.VMEM(out_proj.shape, BF16),
@@ -507,6 +584,7 @@
             pltpu.VMEM((nt * sub, depth), BF16),
             pltpu.VMEM((ns * sub, width), BF16),
             pltpu.VMEM((heads, nt * queries, keys), BF16),
+            pltpu.VMEM((groups, 3, queries, keys // 2), BF16),
             pltpu.VMEM((nt, 1, targets), jnp.int32),
             pltpu.VMEM((1, total), jnp.int32),
             pltpu.VMEM((groups, total, head_dim), BF16),
@@ -521,9 +599,10 @@
             pltpu.VMEM((nt, own, targets), BF16),
             pltpu.VMEM((nt, own, targets), BF16),
             pltpu.VMEM((total, 1), jnp.int32),
-            sem(9),
+            pltpu.SMEM(tile_pattern.shape, jnp.int32),
+            sem(10),
             sem(nt), sem(nt), sem(nt), sem(nt), sem(nt), sem(nt),
-            sem(nt, groups), sem(nt, groups), sem(nt, groups), sem(nt), sem(nt), sem(nt),
+            sem(nt, groups + repeat - 1), sem(nt, groups + repeat - 1), sem(nt, groups + repeat - 1), sem(nt), sem(nt), sem(nt),
             sem(nt, nx), sem(nt, nx), sem(nt, nx), sem(nt, nx),
             sem(nx), sem(nx), sem(nx), sem(nx),
             sem(nt, nx), sem(nt, nx), sem(nt, nx), sem(nt, nx), sem(nt), sem(nt),

time: 52.4 us -> 48.9 us (0.933)
  Pallas kernels: 50.8 us -> 48.1 us
  local copies, waits for them, and re-layouts: 1.38 us -> 0.62 us
    pallas_call x1, Pallas kernels: 50.8 us -> 48.1 us  [resident_shards(): pl.pallas_call(functools.partial(edge_kernel, nt, ns), out_shape=pltpu.VM...]
    unnamed x1, local copies, waits for them, and re-layouts: 1.38 us -> 0.62 us
where the time goes in v2:
time: 48.9 us; the launch traced here: 48.8 us
  Pallas kernels  48.1 us (98%)
  local copies, waits for them, and re-layouts  0.62 us (1%)
    pallas_call x1, Pallas kernels, resident_shards(): pl.pallas_call(functools.partial(edge_kernel, nt, ns), out_shape=pltpu.VM...  48.1 us

profile of v2, /device:TPU:0, one launch (start us, length us, event | category | flops | bytes accessed | tf_op | source)
XLA Modules:
  0.0 48.8 jit_solution(14515039770431190003)
XLA Ops:
  0.0 48.1 %shard_map.82 = bf16[64,256]{1,0:T(8,128)(2,1)S(1)} custom-call(bf16[64,4608]{1,0:T(8,128)(2,1)} %tgt_hbm.1, s32[1,256]{1,0:T(1,128)} %bitcast.2, bf16[16,4608]{1,0:T(8,128)(2,1)} %dec_hbm.1, s32[1,256]{1,0:T(1,128)} %bitcast.3, bf16[8,1152,128]{2,1,0:T(8,128)(2,1)} %oproj_hbm.1, bf16[4,4608,128]{2,1,0:T(8,128)(2,1)} %vproj_hbm.1, ...), custom_call_target="tpu_custom_call" | custom-call | tf_op jit(solution)/shard_map/pallas_call | solution.py:575
  48.1 0.6 %copy.10 = bf16[64,256]{1,0:T(8,128)(2,1)} copy(bf16[64,256]{1,0:T(8,128)(2,1)S(1)} %shard_map.82) | data formatting | bytes 65536

commit v3 on v2

--- a/solution.py
+++ b/solution.py
@@ -159,8 +159,6 @@
     def xsrc(dx):
         return lax.rem(x + dx, nx) * 2 + core
 
-    pending = []
-
     def remote(src, dst, ssem, rsem, axis, index):
         return pltpu.make_async_remote_copy(
             src_ref=src, dst_ref=dst, send_sem=ssem, recv_sem=rsem,
@@ -169,7 +167,6 @@
 
     def send(src, dst, ssem, rsem, axis, index):
         remote(src, dst, ssem, rsem, axis, index).start()
-        pending.append((None, lambda: remote(src, dst, ssem, rsem, axis, index)))
 
     def arrived(dst, rsem):
         remote(dst, dst, local_sem.at[0], rsem, "src", mate).wait_recv()
@@ -232,21 +229,21 @@
         @pl.when(b < lowest)
         def _():
             a, d = view(pl.ds(0, half))
-            act(remote(a, d, ssem.at[b, g], a_r.at[b, g], "tgt", device))
+            act(remote(a, d, ssem.at[0], a_r.at[b, g], "tgt", device))
 
         if packed >= 0 and g < groups:
             @pl.when(b == packed)
             def _():
-                act(remote(packs.at[g], packs.at[g], ssem.at[b, g], a_r.at[b, g], "tgt", device))
+                act(remote(packs.at[g], packs.at[g], ssem.at[0], a_r.at[b, g], "tgt", device))
 
         @pl.when((b >= lowest) & (b != packed))
         def _():
             a, d = view(pl.ds(0, keys))
-            act(remote(a, d, ssem.at[b, g], a_r.at[b, g], "tgt", device))
+            act(remote(a, d, ssem.at[0], a_r.at[b, g], "tgt", device))
 
     def value_copy(b, ssem, device):
         dst = values.at[:, vrow(b), :]
-        return remote(dst, dst, ssem.at[b], v_r.at[b], "tgt", device)
+        return remote(dst, dst, ssem.at[0], v_r.at[b], "tgt", device)
 
     start = lambda copy: copy.start()
     wait_send = lambda copy: copy.wait_send()
@@ -259,16 +256,16 @@
         pl.when(c > 0)(act)
 
     for dx in range(1, nx):
-        send(dec_hbm, decfull.at[drow(s)], xf_s.at[dx], xf_r.at[x], "src", xsrc(dx))
-    send(dec_hbm, decfull.at[drow(s)], cf_s.at[x], cf_r.at[x], "src", mate)
+        send(dec_hbm, decfull.at[drow(s)], xf_s.at[0], xf_r.at[x], "src", xsrc(dx))
+    send(dec_hbm, decfull.at[drow(s)], cf_s.at[0], cf_r.at[x], "src", mate)
     def spread_copies(b):
         return (
-            remote(tgt_hbm.at[:, cols(b)], tslices.at[c, trow(s)], zt_s.at[b], zt_r.at[c], "tgt", b),
-            remote(tpos_hbm, tpos.at[c], zp_s.at[b], zp_r.at[c], "tgt", b),
+            remote(tgt_hbm.at[:, cols(b)], tslices.at[c, trow(s)], zt_s.at[0], zt_r.at[c], "tgt", b),
+            remote(tpos_hbm, tpos.at[c], zp_s.at[0], zp_r.at[c], "tgt", b),
         )
 
     def slice_copy(b):
-        return remote(dec_hbm.at[:, cols(b)], dslices.at[drow(c)], zd_s.at[b], zd_r.at[c], "tgt", b)
+        return remote(dec_hbm.at[:, cols(b)], dslices.at[drow(c)], zd_s.at[0], zd_r.at[0], "tgt", b)
 
     def send_slices():
         for j in range(1, nt):
@@ -282,8 +279,8 @@
     spread(1)
     spread(2)
     for dx in range(1, nx):
-        send(tgt_hbm.at[:, cols(c)], tslices.at[c, trow(s)], xt_s.at[c, dx], xt_r.at[c, x], "src", xsrc(dx))
-    send(tgt_hbm.at[:, cols(c)], tslices.at[c, trow(s)], ct_s.at[c, x], ct_r.at[c, x], "src", mate)
+        send(tgt_hbm.at[:, cols(c)], tslices.at[c, trow(s)], xt_s.at[0], xt_r.at[c, x], "src", xsrc(dx))
+    send(tgt_hbm.at[:, cols(c)], tslices.at[c, trow(s)], ct_s.at[0], ct_r.at[c, x], "src", mate)
 
     fetch[1].wait()
     fetch[2].wait()
@@ -320,15 +317,15 @@
         b = order[j]
         arrived(tslices.at[b, trow(s)], zt_r.at[b])
         for dx in range(1, nx):
-            send(tslices.at[b, trow(s)], tslices.at[b, trow(s)], xt_s.at[b, dx], xt_r.at[b, x], "src", xsrc(dx))
-        send(tslices.at[b, trow(s)], tslices.at[b, trow(s)], ct_s.at[b, x], ct_r.at[b, x], "src", mate)
+            send(tslices.at[b, trow(s)], tslices.at[b, trow(s)], xt_s.at[0], xt_r.at[b, x], "src", xsrc(dx))
+        send(tslices.at[b, trow(s)], tslices.at[b, trow(s)], ct_s.at[0], ct_r.at[b, x], "src", mate)
 
     fetch[0].wait()
     for dx in range(1, nx):
         z = lax.rem(x + dx, nx)
         y = xsrc(dx)
         arrived(decfull.at[drow(y)], xf_r.at[z])
-        send(decfull.at[drow(y)], decfull.at[drow(y)], cf_s.at[z], cf_r.at[z], "src", mate)
+        send(decfull.at[drow(y)], decfull.at[drow(y)], cf_s.at[0], cf_r.at[z], "src", mate)
     for dx in range(nx):
         z = lax.rem(x + dx, nx)
         arrived(decfull.at[drow(z * 2 + 1 - core)], cf_r.at[z])
@@ -358,7 +355,7 @@
             z = lax.rem(x + dx, nx)
             y = z * 2 + core
             arrived(tslices.at[b, trow(y)], xt_r.at[b, z])
-            send(tslices.at[b, trow(y)], tslices.at[b, trow(y)], ct_s.at[b, z], ct_r.at[b, z], "src", mate)
+            send(tslices.at[b, trow(y)], tslices.at[b, trow(y)], ct_s.at[0], ct_r.at[b, z], "src", mate)
 
     def ready(j):
         b = order[j]
@@ -387,8 +384,7 @@
 
     def wait_slices():
         fetch[5].wait()
-        for j in range(1, nt):
-            arrived(dslices.at[drow(order[j])], zd_r.at[order[j]])
+        arrived(dslices.at[:(nt - 1) * sub], zd_r.at[0])
 
     def add_direct(b):
         direct = dot_nt(dslices[...], tslices[b])
@@ -435,14 +431,14 @@
 
     def to_mate(b):
         for z in range(nx):
-            send(edges.at[b, erow(z * 2 + 1 - core)], core_in.at[b, z], ce_s.at[b, z], ce_r.at[b, z], "src", mate)
+            send(edges.at[b, erow(z * 2 + 1 - core)], core_in.at[b, z], ce_s.at[0], ce_r.at[b, z], "src", mate)
 
     def over_x(b):
         for dx in range(1, nx):
             z = lax.rem(x + dx, nx)
             arrived(core_in.at[b, z], ce_r.at[b, z])
             x_out[b, z] = (edges[b, erow(z * 2 + core)] + core_in[b, z]).astype(BF16)
-            send(x_out.at[b, z], x_in.at[b, x], xe_s.at[b, z], xe_r.at[b, x], "src", z * 2 + core)
+            send(x_out.at[b, z], x_in.at[b, x], xe_s.at[0], xe_r.at[b, x], "src", z * 2 + core)
         arrived(core_in.at[b, x], ce_r.at[b, x])
 
     def over_z(b, away):
@@ -453,7 +449,7 @@
             mine += x_in[b, z].astype(F32)
         if away:
             z_out[b] = mine.astype(BF16)
-            send(z_out.at[b], z_in.at[c], ze_s.at[b], ze_r.at[c], "tgt", b)
+            send(z_out.at[b], z_in.at[c], ze_s.at[0], ze_r.at[0], "tgt", b)
         return mine
 
     spread(3)
@@ -529,28 +525,36 @@
         over_z(last_of[j], True)
     mine = over_z(c, False)
     fetch[8].wait()
+    def drained(view, ssem):
+        remote(view, view, ssem.at[0], local_sem.at[0], "src", mate).wait_send()
+
+    drained(tslices.at[:nt - 1, :rows], zt_s)
+    drained(tslices.at[:, :(nx - 1) * rows], xt_s)
+    drained(tslices.at[:, :nx * rows], ct_s)
+    drained(dslices.at[:(nt - 1) * sub], zd_s)
+    drained(tpos.at[:nt - 1], zp_s)
+    drained(decfull.at[:(nx - 1) * sub], xf_s)
+    drained(decfull.at[:nx * sub], cf_s)
+    drained(core_in, ce_s)
+    drained(x_out.at[:, :nx - 1], xe_s)
+    drained(z_out.at[:nt - 1], ze_s)
+
+    def tiles(b):
+        return heads if b < lowest else 3 * groups if b == packed else 2 * heads
+
+    for i in range(nt):
+        @pl.when(c == i)
+        def _():
+            if i + 1 < nt:
+                drained(vproj.at[0, :queries * sum(tiles(b) for b in range(i + 1))], ar_s)
+                drained(values.at[:, :(i + 1) * block], vr_s)
+            if i > 0:
+                drained(vproj.at[0, :queries * sum(tiles(b) for b in range(i, nt))], al_s)
+                drained(values.at[:, :(nt - i) * block], vl_s)
+
+    arrived(z_in.at[:nt - 1], ze_r.at[0])
     for j in range(1, nt):
-        for copy in spread_copies(order[j]) + (slice_copy(order[j]),):
-            copy.wait_send()
-    for _, again in pending:
-        again().wait_send()
-    for k in range(nt):
-        @pl.when((c - k >= 0) & (c + 1 < nt))
-        def _():
-            for g in range(len(chunks)):
-                attn_copy(c - k, g, ar_s, c + 1, wait_send)
-            value_copy(c - k, vr_s, c + 1).wait_send()
-
-        @pl.when((c + k < nt) & (c > 0))
-        def _():
-            for g in range(len(chunks)):
-                attn_copy(c + k, g, al_s, c - 1, wait_send)
-            value_copy(c + k, vl_s, c - 1).wait_send()
-
-    for j in range(1, nt):
-        b = order[j]
-        arrived(z_in.at[b], ze_r.at[b])
-        mine += z_in[b].astype(F32)
+        mine += z_in[order[j]].astype(F32)
     kept = pat_ref[(s * own) // block, c]
     out_ref[...] = (mine * kept.astype(F32)).astype(BF16)
 
@@ -601,11 +605,11 @@
             pltpu.VMEM((total, 1), jnp.int32),
             pltpu.SMEM(tile_pattern.shape, jnp.int32),
             sem(10),
-            sem(nt), sem(nt), sem(nt), sem(nt), sem(nt), sem(nt),
-            sem(nt, groups + repeat - 1), sem(nt, groups + repeat - 1), sem(nt, groups + repeat - 1), sem(nt), sem(nt), sem(nt),
-            sem(nt, nx), sem(nt, nx), sem(nt, nx), sem(nt, nx),
-            sem(nx), sem(nx), sem(nx), sem(nx),
-            sem(nt, nx), sem(nt, nx), sem(nt, nx), sem(nt, nx), sem(nt), sem(nt),
+            sem(1), sem(nt), sem(1), sem(1), sem(1), sem(nt),
+            sem(1), sem(1), sem(nt, groups + repeat - 1), sem(1), sem(1), sem(nt),
+            sem(1), sem(nt, nx), sem(1), sem(nt, nx),
+            sem(1), sem(nx), sem(1), sem(nx),
+            sem(1), sem(nt, nx), sem(1), sem(nt, nx), sem(1), sem(1),
         ],
         compiler_params=pltpu.CompilerParams(
             collective_id=0, has_side_effects=True, vmem_limit_bytes=60 * 1024 * 1024
@@ -634,6 +638,9 @@
     fits = (
         depth % 128 == 0 and head_dim == 128 and ns % 2 == 0 and nt > 2
         and decoder_rows.shape[0] % 16 == 0 and attention.shape[1] % 16 == 0
+        and attention.shape[2] == 2 * head_dim and nt == 4
+        and value_proj.shape[0] == 4 and heads == 8
+        and 2 * heads * attention.shape[1] * nt <= target_rows.shape[1]
         and need < 40 * 1024 * 1024
     )
     plan = resident_shards if fits else gathered_shards

time: 48.9 us -> 48.1 us (0.984)
  Pallas kernels: 48.1 us -> 47.3 us
    pallas_call x1, Pallas kernels: 48.1 us -> 47.3 us  [resident_shards(): pl.pallas_call(functools.partial(edge_kernel, nt, ns), out_shape=pltpu.VM...]
where the time goes in v3:
time: 48.1 us; the launch traced here: 47.9 us
  Pallas kernels  47.3 us (98%)
  local copies, waits for them, and re-layouts  0.62 us (1%)
    pallas_call x1, Pallas kernels, resident_shards(): pl.pallas_call(functools.partial(edge_kernel, nt, ns), out_shape=pltpu.VM...  47.3 us

profile of v3, /device:TPU:0, one launch (start us, length us, event | category | flops | bytes accessed | tf_op | source)
XLA Modules:
  0.0 47.9 jit_solution(13679058732685520572)
XLA Ops:
  0.0 47.3 %shard_map.82 = bf16[64,256]{1,0:T(8,128)(2,1)S(1)} custom-call(bf16[64,4608]{1,0:T(8,128)(2,1)} %tgt_hbm.1, s32[1,256]{1,0:T(1,128)} %bitcast.2, bf16[16,4608]{1,0:T(8,128)(2,1)} %dec_hbm.1, s32[1,256]{1,0:T(1,128)} %bitcast.3, bf16[8,1152,128]{2,1,0:T(8,128)(2,1)} %oproj_hbm.1, bf16[4,4608,128]{2,1,0:T(8,128)(2,1)} %vproj_hbm.1, ...), custom_call_target="tpu_custom_call" | custom-call | tf_op jit(solution)/shard_map/pallas_call | solution.py:579
  47.3 0.6 %copy.10 = bf16[64,256]{1,0:T(8,128)(2,1)} copy(bf16[64,256]{1,0:T(8,128)(2,1)S(1)} %shard_map.82) | data formatting | bytes 65536

commit v4 on v3

--- a/solution.py
+++ b/solution.py
@@ -257,7 +257,7 @@
 
     for dx in range(1, nx):
         send(dec_hbm, decfull.at[drow(s)], xf_s.at[0], xf_r.at[x], "src", xsrc(dx))
-    send(dec_hbm, decfull.at[drow(s)], cf_s.at[0], cf_r.at[x], "src", mate)
+    send(dec_hbm, decfull.at[drow(s)], cf_s.at[0], cf_r.at[0], "src", mate)
     def spread_copies(b):
         return (
             remote(tgt_hbm.at[:, cols(b)], tslices.at[c, trow(s)], zt_s.at[0], zt_r.at[c], "tgt", b),
@@ -280,7 +280,7 @@
     spread(2)
     for dx in range(1, nx):
         send(tgt_hbm.at[:, cols(c)], tslices.at[c, trow(s)], xt_s.at[0], xt_r.at[c, x], "src", xsrc(dx))
-    send(tgt_hbm.at[:, cols(c)], tslices.at[c, trow(s)], ct_s.at[0], ct_r.at[c, x], "src", mate)
+    send(tgt_hbm.at[:, cols(c)], tslices.at[c, trow(s)], ct_s.at[0], ct_r.at[c], "src", mate)
 
     fetch[1].wait()
     fetch[2].wait()
@@ -318,17 +318,15 @@
         arrived(tslices.at[b, trow(s)], zt_r.at[b])
         for dx in range(1, nx):
             send(tslices.at[b, trow(s)], tslices.at[b, trow(s)], xt_s.at[0], xt_r.at[b, x], "src", xsrc(dx))
-        send(tslices.at[b, trow(s)], tslices.at[b, trow(s)], ct_s.at[0], ct_r.at[b, x], "src", mate)
+        send(tslices.at[b, trow(s)], tslices.at[b, trow(s)], ct_s.at[0], ct_r.at[b], "src", mate)
 
     fetch[0].wait()
     for dx in range(1, nx):
         z = lax.rem(x + dx, nx)
         y = xsrc(dx)
         arrived(decfull.at[drow(y)], xf_r.at[z])
-        send(decfull.at[drow(y)], decfull.at[drow(y)], cf_s.at[0], cf_r.at[z], "src", mate)
-    for dx in range(nx):
-        z = lax.rem(x + dx, nx)
-        arrived(decfull.at[drow(z * 2 + 1 - core)], cf_r.at[z])
+        send(decfull.at[drow(y)], decfull.at[drow(y)], cf_s.at[0], cf_r.at[0], "src", mate)
+    arrived(decfull.at[:nx * sub], cf_r.at[0])
     fetch[3].wait()
 
     @pl.loop(0, groups)
@@ -355,7 +353,7 @@
             z = lax.rem(x + dx, nx)
             y = z * 2 + core
             arrived(tslices.at[b, trow(y)], xt_r.at[b, z])
-            send(tslices.at[b, trow(y)], tslices.at[b, trow(y)], ct_s.at[0], ct_r.at[b, z], "src", mate)
+            send(tslices.at[b, trow(y)], tslices.at[b, trow(y)], ct_s.at[0], ct_r.at[b], "src", mate)
 
     def ready(j):
         b = order[j]
@@ -364,9 +362,7 @@
             fetch[6].wait()
         else:
             arrived(tpos.at[b], zp_r.at[b])
-        for dx in range(nx):
-            z = lax.rem(x + dx, nx)
-            arrived(tslices.at[b, trow(z * 2 + 1 - core)], ct_r.at[b, z])
+        arrived(tslices.at[b, :nx * rows], ct_r.at[b])
 
     def read_block(j, part):
         b = order[j]
@@ -431,15 +427,14 @@
 
     def to_mate(b):
         for z in range(nx):
-            send(edges.at[b, erow(z * 2 + 1 - core)], core_in.at[b, z], ce_s.at[0], ce_r.at[b, z], "src", mate)
+            send(edges.at[b, erow(z * 2 + 1 - core)], core_in.at[b, z], ce_s.at[0], ce_r.at[b], "src", mate)
 
     def over_x(b):
+        arrived(core_in.at[b], ce_r.at[b])
         for dx in range(1, nx):
             z = lax.rem(x + dx, nx)
-            arrived(core_in.at[b, z], ce_r.at[b, z])
             x_out[b, z] = (edges[b, erow(z * 2 + core)] + core_in[b, z]).astype(BF16)
             send(x_out.at[b, z], x_in.at[b, x], xe_s.at[0], xe_r.at[b, x], "src", z * 2 + core)
-        arrived(core_in.at[b, x], ce_r.at[b, x])
 
     def over_z(b, away):
         mine = edges[b, erow(s)] + core_in[b, x]
@@ -464,8 +459,8 @@
     ready(0)
     take(3)
     issue(3)
+    ready(1)
     read_block(0, 1)
-    ready(1)
     read_block(1, 0)
     attn_step(1, 0)
     issue(4)
@@ -479,17 +474,18 @@
     ready(2)
     attn_step(2, 0)
     read_block(2, 1)
-    send_slices()
+    pl.when(jnp.logical_not(inner))(send_slices)
+    pl.when(inner)(send_slices)
     cross(3)
     value_step(3)
     attn_step(2, 1)
+    attn_step(1, 4)
     read_block(2, 0)
     ready(3)
     read_block(3, 1)
     attn_step(3, 0)
     pick_keys(0)
     read_block(3, 0)
-    attn_step(1, 4)
     mix_all(0)
     attn_step(2, 2)
     attn_step(3, 1)
@@ -607,9 +603,9 @@
             sem(10),
             sem(1), sem(nt), sem(1), sem(1), sem(1), sem(nt),
             sem(1), sem(1), sem(nt, groups + repeat - 1), sem(1), sem(1), sem(nt),
-            sem(1), sem(nt, nx), sem(1), sem(nt, nx),
-            sem(1), sem(nx), sem(1), sem(nx),
-            sem(1), sem(nt, nx), sem(1), sem(nt, nx), sem(1), sem(1),
+            sem(1), sem(nt, nx), sem(1), sem(nt),
+            sem(1), sem(nx), sem(1), sem(1),
+            sem(1), sem(nt), sem(1), sem(nt, nx), sem(1), sem(1),
         ],
         compiler_params=pltpu.CompilerParams(
             collective_id=0, has_side_effects=True, vmem_limit_bytes=60 * 1024 * 1024

time: 48.1 us -> 47.5 us (0.988)
  Pallas kernels: 47.3 us -> 46.7 us
    pallas_call x1, Pallas kernels: 47.3 us -> 46.7 us  [resident_shards(): pl.pallas_call(functools.partial(edge_kernel, nt, ns), out_shape=pltpu.VM...]
where the time goes in v4:
time: 47.5 us; the launch traced here: 47.3 us
  Pallas kernels  46.7 us (98%)
  local copies, waits for them, and re-layouts  0.62 us (1%)
    pallas_call x1, Pallas kernels, resident_shards(): pl.pallas_call(functools.partial(edge_kernel, nt, ns), out_shape=pltpu.VM...  46.7 us

profile of v4, /device:TPU:0, one launch (start us, length us, event | category | flops | bytes accessed | tf_op | source)
XLA Modules:
  0.0 47.3 jit_solution(10619039703023549487)
XLA Ops:
  0.0 46.7 %shard_map.82 = bf16[64,256]{1,0:T(8,128)(2,1)S(1)} custom-call(bf16[64,4608]{1,0:T(8,128)(2,1)} %tgt_hbm.1, s32[1,256]{1,0:T(1,128)} %bitcast.2, bf16[16,4608]{1,0:T(8,128)(2,1)} %dec_hbm.1, s32[1,256]{1,0:T(1,128)} %bitcast.3, bf16[8,1152,128]{2,1,0:T(8,128)(2,1)} %oproj_hbm.1, bf16[4,4608,128]{2,1,0:T(8,128)(2,1)} %vproj_hbm.1, ...), custom_call_target="tpu_custom_call" | custom-call | tf_op jit(solution)/shard_map/pallas_call | solution.py:575
  46.7 0.6 %copy.10 = bf16[64,256]{1,0:T(8,128)(2,1)} copy(bf16[64,256]{1,0:T(8,128)(2,1)S(1)} %shard_map.82) | data formatting | bytes 65536

commit v5 on v4

--- a/solution.py
+++ b/solution.py
@@ -256,7 +256,7 @@
         pl.when(c > 0)(act)
 
     for dx in range(1, nx):
-        send(dec_hbm, decfull.at[drow(s)], xf_s.at[0], xf_r.at[x], "src", xsrc(dx))
+        send(dec_hbm, decfull.at[drow(s)], xf_s.at[0], xf_r.at[dx - 1], "src", xsrc(dx))
     send(dec_hbm, decfull.at[drow(s)], cf_s.at[0], cf_r.at[0], "src", mate)
     def spread_copies(b):
         return (
@@ -279,7 +279,7 @@
     spread(1)
     spread(2)
     for dx in range(1, nx):
-        send(tgt_hbm.at[:, cols(c)], tslices.at[c, trow(s)], xt_s.at[0], xt_r.at[c, x], "src", xsrc(dx))
+        send(tgt_hbm.at[:, cols(c)], tslices.at[c, trow(s)], xt_s.at[0], xt_r.at[c, dx - 1], "src", xsrc(dx))
     send(tgt_hbm.at[:, cols(c)], tslices.at[c, trow(s)], ct_s.at[0], ct_r.at[c], "src", mate)
 
     fetch[1].wait()
@@ -317,14 +317,14 @@
         b = order[j]
         arrived(tslices.at[b, trow(s)], zt_r.at[b])
         for dx in range(1, nx):
-            send(tslices.at[b, trow(s)], tslices.at[b, trow(s)], xt_s.at[0], xt_r.at[b, x], "src", xsrc(dx))
+            send(tslices.at[b, trow(s)], tslices.at[b, trow(s)], xt_s.at[0], xt_r.at[b, dx - 1], "src", xsrc(dx))
         send(tslices.at[b, trow(s)], tslices.at[b, trow(s)], ct_s.at[0], ct_r.at[b], "src", mate)
 
     fetch[0].wait()
     for dx in range(1, nx):
         z = lax.rem(x + dx, nx)
         y = xsrc(dx)
-        arrived(decfull.at[drow(y)], xf_r.at[z])
+        arrived(decfull.at[drow(y)], xf_r.at[nx - 1 - dx])
         send(decfull.at[drow(y)], decfull.at[drow(y)], cf_s.at[0], cf_r.at[0], "src", mate)
     arrived(decfull.at[:nx * sub], cf_r.at[0])
     fetch[3].wait()
@@ -352,7 +352,7 @@
         for dx in range(1, nx):
             z = lax.rem(x + dx, nx)
             y = z * 2 + core
-            arrived(tslices.at[b, trow(y)], xt_r.at[b, z])
+            arrived(tslices.at[b, trow(y)], xt_r.at[b, nx - 1 - dx])
             send(tslices.at[b, trow(y)], tslices.at[b, trow(y)], ct_s.at[0], ct_r.at[b], "src", mate)
 
     def ready(j):
@@ -434,13 +434,13 @@
         for dx in range(1, nx):
             z = lax.rem(x + dx, nx)
             x_out[b, z] = (edges[b, erow(z * 2 + core)] + core_in[b, z]).astype(BF16)
-            send(x_out.at[b, z], x_in.at[b, x], xe_s.at[0], xe_r.at[b, x], "src", z * 2 + core)
+            send(x_out.at[b, z], x_in.at[b, x], xe_s.at[0], xe_r.at[b, dx - 1], "src", z * 2 + core)
 
     def over_z(b, away):
         mine = edges[b, erow(s)] + core_in[b, x]
         for dx in range(1, nx):
             z = lax.rem(x + dx, nx)
-            arrived(x_in.at[b, z], xe_r.at[b, z])
+            arrived(x_in.at[b, z], xe_r.at[b, nx - 1 - dx])
             mine += x_in[b, z].astype(F32)
         if away:
             z_out[b] = mine.astype(BF16)
@@ -603,9 +603,9 @@
             sem(10),
             sem(1), sem(nt), sem(1), sem(1), sem(1), sem(nt),
             sem(1), sem(1), sem(nt, groups + repeat - 1), sem(1), sem(1), sem(nt),
-            sem(1), sem(nt, nx), sem(1), sem(nt),
-            sem(1), sem(nx), sem(1), sem(1),
-            sem(1), sem(nt), sem(1), sem(nt, nx), sem(1), sem(1),
+            sem(1), sem(nt, nx - 1), sem(1), sem(nt),
+            sem(1), sem(nx - 1), sem(1), sem(1),
+            sem(1), sem(nt), sem(1), sem(nt, nx - 1), sem(1), sem(1),
         ],
         compiler_params=pltpu.CompilerParams(
             collective_id=0, has_side_effects=True, vmem_limit_bytes=60 * 1024 * 1024
@@ -632,7 +632,7 @@
         source_pos.shape[0], target_pos.shape[0],
     )
     fits = (
-        depth % 128 == 0 and head_dim == 128 and ns % 2 == 0 and nt > 2
+        depth % 128 == 0 and head_dim == 128 and ns % 2 == 0 and ns > 2 and nt > 2
         and decoder_rows.shape[0] % 16 == 0 and attention.shape[1] % 16 == 0
         and attention.shape[2] == 2 * head_dim and nt == 4
         and value_proj.shape[0] == 4 and heads == 8

time: 47.5 us -> 47.4 us (level)
  no operation moved by 1% of the time
where the time goes in v5:
time: 47.4 us; the launch traced here: 47.3 us
  Pallas kernels  46.6 us (98%)
  local copies, waits for them, and re-layouts  0.62 us (1%)
    pallas_call x1, Pallas kernels, resident_shards(): pl.pallas_call(functools.partial(edge_kernel, nt, ns), out_shape=pltpu.VM...  46.6 us

profile of v5, /device:TPU:0, one launch (start us, length us, event | category | flops | bytes accessed | tf_op | source)
XLA Modules:
  0.0 47.3 jit_solution(852289132229595860)
XLA Ops:
  0.0 46.6 %shard_map.82 = bf16[64,256]{1,0:T(8,128)(2,1)S(1)} custom-call(bf16[64,4608]{1,0:T(8,128)(2,1)} %tgt_hbm.1, s32[1,256]{1,0:T(1,128)} %bitcast.2, bf16[16,4608]{1,0:T(8,128)(2,1)} %dec_hbm.1, s32[1,256]{1,0:T(1,128)} %bitcast.3, bf16[8,1152,128]{2,1,0:T(8,128)(2,1)} %oproj_hbm.1, bf16[4,4608,128]{2,1,0:T(8,128)(2,1)} %vproj_hbm.1, ...), custom_call_target="tpu_custom_call" | custom-call | tf_op jit(solution)/shard_map/pallas_call | solution.py:575
  46.6 0.6 %copy.10 = bf16[64,256]{1,0:T(8,128)(2,1)} copy(bf16[64,256]{1,0:T(8,128)(2,1)S(1)} %shard_map.82) | data formatting | bytes 65536
